TPU v7x, 32 devices: a whole 2x2x4 slice. The times are simulated.
32 devices in a mesh: gx: 4 (over y, x), gy: 4 (over z), gz: 2 (over core).
Axes of the slice: x: 2, y: 2, z: 4, core: 2. Of those that a mesh axis runs over, the one named last changes fastest.
Arguments:
- positions: float32 [12, 12, 16, 96], P('gx', 'gy', 'gz'), may hold values from 0 to 1
- types: int32 [12, 12, 16, 32], P('gx', 'gy', 'gz'), may hold values from 0 to 2
Outputs:
- forces_energy: float32 [12, 12, 16, 128], P('gx', 'gy', 'gz')
Inputs may be any that keep to these rules, and one draw needn't show every extreme that they name: `types`: 0 marks an empty slot, 1 a copper atom, 2 a nickel atom.
All inputs are finite; a program needn't handle non-finite values.
Results may differ from a plain program's by a relative error of at most 0.0001.
Values sent between devices are 32-bit elements; how exact they have to be, the bound alone decides.
A program may use at most 64 MiB of HBM per device.

v0:
```python
import jax
import jax.numpy as jnp
from jax import lax
from jax.sharding import PartitionSpec as P

cut_square = 0.9025
density_rate = 3.0
pair_rate = 6.0


def padded_2(value, sides, width):
    for axis, dim in sides:
        peers, length = (lax.axis_size(axis), value.shape[dim])
        up = [(i, (i + 1) % peers) for i in range(peers)]
        down = [(j, i) for i, j in up]
        last = lax.slice_in_dim(value, length - width, length, axis=dim)
        first = lax.slice_in_dim(value, 0, width, axis=dim)
        before = lax.ppermute(last, axis, up)
        after = lax.ppermute(first, axis, down)
        value = jnp.concatenate([before, value, after], axis=dim)
    return value


def type_tables(types):
    weight = jnp.where(types == 1, 1.0, jnp.where(types == 2, 1.6, 0.0)).astype(jnp.float32)
    embedding = jnp.where(types == 1, 1.0, jnp.where(types == 2, 1.4, 0.0)).astype(jnp.float32)
    return (weight, embedding)


def separation(own_coords, other_coords, cell_shift):
    shift_vector = jnp.asarray(cell_shift, jnp.float32).reshape(3, 1, 1)
    displace = shift_vector + other_coords[..., :, None, :] - own_coords[..., :, :, None]
    return (displace, jnp.sum(displace * displace, axis=-3))


def density_shape(square):
    margin = jnp.maximum(1.0 - square / cut_square, 0.0)
    return jnp.exp(-density_rate * square) * margin * margin


def all_shapes(square):
    margin = jnp.maximum(1.0 - square / cut_square, 0.0)
    density_exponent = jnp.exp(-density_rate * square)
    pair_exp = jnp.exp(-pair_rate * square)
    dens_slope = -density_exponent * margin * (density_rate * margin + 2.0 / cut_square)
    pair_value = pair_exp * margin * margin
    pair_slope = -pair_exp * margin * (pair_rate * margin + 2.0 / cut_square)
    return (dens_slope, pair_value, pair_slope)


def half_shifts():
    upward = [
        (a, b, c) for a in (-1, 0, 1) for b in (-1, 0, 1) for c in (-1, 0, 1) if a + b + c > 0
    ]
    return [(0, 0, 0)] + upward + [(1, -1, 0), (0, 1, -1), (-1, 0, 1)]


def fold_classes():
    return [(0,), (1,), (2,), (0, 1), (0, 2), (1, 2), (0, 1, 2)]


def class_fold(block, members):
    for axis_index in range(3):
        inner = block.shape[axis_index] - 2
        if axis_index in members:
            lower = lax.slice_in_dim(block, 0, 1, axis=axis_index)
            upper = lax.slice_in_dim(block, inner + 1, inner + 2, axis=axis_index)
            middle_shape = list(block.shape)
            middle_shape[axis_index] = inner - 2
            middle = jnp.zeros(tuple(middle_shape), block.dtype)
            block = jnp.concatenate([lower, middle, upper], axis=axis_index)
        else:
            block = lax.slice_in_dim(block, 1, inner + 1, axis=axis_index)
    return block


def build_transfer_array(neighbour_image_block):
    return jnp.concatenate(
        [class_fold(neighbour_image_block, members) for members in fold_classes()], axis=3
    )


def collect_back(incoming_atoms, width):
    summed = None
    for index, members in enumerate(fold_classes()):
        piece = class_fold(incoming_atoms[..., index * width : (index + 1) * width], members)
        summed = piece if summed is None else summed + piece
    return summed


def row_of(array, index):
    return lax.dynamic_index_in_dim(array, index, 0, keepdims=False)


def put_row(array, index, value):
    return lax.dynamic_update_index_in_dim(array, value, index, 0)


def add_row(array, index, value):
    return put_row(array, index, row_of(array, index) + value)


def body(positions, types):
    cell_count_first, cells_y, cells_z, slots = types.shape
    weight, embedding = type_tables(types)
    payload = jnp.concatenate([positions, weight], axis=3)
    padded = padded_2(payload, (("gx", 0), ("gy", 1), ("gz", 2)), 1)
    pad_coords = padded[..., : 3 * slots].reshape(
        cell_count_first + 2, cells_y + 2, cells_z + 2, 3, slots
    )
    pad_weight = padded[..., 3 * slots :]
    own_coords = positions.reshape(cell_count_first, cells_y, cells_z, 3, slots)
    slot_ids = lax.broadcasted_iota(jnp.int32, (slots, slots), 0)
    pair_ids = lax.broadcasted_iota(jnp.int32, (slots, slots), 1)
    ordered = jnp.where(slot_ids < pair_ids, 1.0, 0.0).astype(jnp.float32)

    def window(array, plane, cell_shift):
        layer = row_of(array, plane + 1 + cell_shift[0])
        return layer[
            1 + cell_shift[1] : 1 + cell_shift[1] + cells_y,
            1 + cell_shift[2] : 1 + cell_shift[2] + cells_z,
        ]

    def place(array, cell_shift):
        widths = (
            (1 + cell_shift[1], 1 - cell_shift[1]),
            (1 + cell_shift[2], 1 - cell_shift[2]),
        ) + ((0, 0),) * (array.ndim - 2)
        return jnp.pad(array, widths)

    def half_density_step(plane, carry):
        own_part, image_portion = carry
        plane_coords = row_of(own_coords, plane)
        plane_weight = row_of(weight, plane)
        summed = jnp.zeros((cells_y, cells_z, slots), jnp.float32)
        for cell_shift in half_shifts():
            displace, square = separation(
                plane_coords, window(pad_coords, plane, cell_shift), cell_shift
            )
            dens = density_shape(square)
            if cell_shift == (0, 0, 0):
                dens = dens * ordered
            summed = summed + jnp.sum(
                dens * window(pad_weight, plane, cell_shift)[..., None, :], axis=-1
            )
            image_portion = add_row(
                image_portion,
                plane + 1 + cell_shift[0],
                place(jnp.sum(dens * plane_weight[..., :, None], axis=-2), cell_shift),
            )
        return (put_row(own_part, plane, summed), image_portion)

    start = (
        jnp.zeros((cell_count_first, cells_y, cells_z, slots), jnp.float32),
        jnp.zeros((cell_count_first + 2, cells_y + 2, cells_z + 2, slots), jnp.float32),
    )
    own_part, image_portion = lax.fori_loop(0, cell_count_first, half_density_step, start)
    incoming_atoms = padded_2(
        build_transfer_array(image_portion), (("gx", 0), ("gy", 1), ("gz", 2)), 1
    )
    density_sum = own_part + image_portion[1:-1, 1:-1, 1:-1] + collect_back(incoming_atoms, slots)
    root_value = jnp.sqrt(density_sum + 1.0)
    slope = -embedding / (2.0 * root_value)
    pad_slope = padded_2(slope, (("gx", 0), ("gy", 1), ("gz", 2)), 1)

    def pair_terms(plane, cell_shift):
        plane_weight = row_of(weight, plane)
        plane_slope = row_of(slope, plane)
        other_weight = window(pad_weight, plane, cell_shift)
        other_slope = window(pad_slope, plane, cell_shift)
        displace, square = separation(
            row_of(own_coords, plane), window(pad_coords, plane, cell_shift), cell_shift
        )
        dens_slope, pair_value, pair_slope = all_shapes(square)
        both_weight = plane_weight[..., :, None] * other_weight[..., None, :]
        coupling = (
            plane_slope[..., :, None] * other_weight[..., None, :]
            + other_slope[..., None, :] * plane_weight[..., :, None]
        ) * dens_slope + 0.5 * both_weight * pair_slope
        return (displace, coupling, 0.25 * both_weight * pair_value)

    emb_energy = -embedding * root_value
    force_start = jnp.zeros((cell_count_first, cells_y, cells_z, 3, slots), jnp.float32)
    pair_start = jnp.zeros((cell_count_first, cells_y, cells_z, slots), jnp.float32)

    def half_force_step(plane, carry):
        force_all, pair_all, image_portion = carry
        force_sum = jnp.zeros((cells_y, cells_z, 3, slots), jnp.float32)
        pair_sum = jnp.zeros((cells_y, cells_z, slots), jnp.float32)
        for cell_shift in half_shifts():
            displace, coupling, energy_pair = pair_terms(plane, cell_shift)
            if cell_shift == (0, 0, 0):
                coupling = coupling * ordered
                energy_pair = energy_pair * ordered
            pair_force = 2.0 * coupling[..., None, :, :] * displace
            force_sum = force_sum + jnp.sum(pair_force, axis=-1)
            pair_sum = pair_sum + jnp.sum(energy_pair, axis=-1)
            partner = jnp.concatenate(
                [-jnp.sum(pair_force, axis=-2), jnp.sum(energy_pair, axis=-2)[..., None, :]],
                axis=-2,
            )
            image_portion = add_row(
                image_portion, plane + 1 + cell_shift[0], place(partner, cell_shift)
            )
        return (
            put_row(force_all, plane, force_sum),
            put_row(pair_all, plane, pair_sum),
            image_portion,
        )

    image_start = jnp.zeros((cell_count_first + 2, cells_y + 2, cells_z + 2, 4, slots), jnp.float32)
    force_all, pair_all, image_portion = lax.fori_loop(
        0, cell_count_first, half_force_step, (force_start, pair_start, image_start)
    )
    image_flattened = image_portion.reshape(
        cell_count_first + 2, cells_y + 2, cells_z + 2, 4 * slots
    )
    incoming_atoms = padded_2(
        build_transfer_array(image_flattened), (("gx", 0), ("gy", 1), ("gz", 2)), 1
    )
    own_flat = jnp.concatenate(
        [force_all.reshape(cell_count_first, cells_y, cells_z, 3 * slots), pair_all + emb_energy],
        axis=-1,
    )
    return own_flat + image_flattened[1:-1, 1:-1, 1:-1] + collect_back(incoming_atoms, 4 * slots)


def solution(mesh):
    in_specs = (P("gx", "gy", "gz", None), P("gx", "gy", "gz", None))
    out_specs = P("gx", "gy", "gz", None)
    return jax.shard_map(body, mesh=mesh, in_specs=in_specs, out_specs=out_specs, check_vma=False)
```

profile of v0, /device:TPU:0, one launch (start us, length us, event | category | flops | bytes accessed | tf_op | source)
XLA Modules:
  0.0 152.7 jit_solution(15879694539840778715)
XLA Ops:
  1.6 3.0 %collective-permute-start = (f32[1,3,8,128]{3,2,1,0:T(8,128)S(1)}, f32[1,3,8,128]{3,2,1,0:T(8,128)S(1)}, u32[]{:S(2)}, u32[]{:S(2)}) collective-permute-start(f32[1,3,8,128]{3,2,1,0:T(8,128)S(1)} %get-tuple-element.2066), channel_id=1, source_target_pairs={{0,8},{8,16},{16,24},{24,0},{1,9},{9,17},{17,25},{25,1},{2,10},{10... | collective-permute-start | bytes 36872 | tf_op jit(solution)/shard_map/ppermute | solution.py:18
  10.6 2.2 %collective-permute-start.3 = (f32[5,1,8,128]{3,2,1,0:T(8,128)S(1)}, f32[5,1,8,128]{3,2,1,0:T(8,128)S(1)}, u32[]{:S(2)}, u32[]{:S(2)}) collective-permute-start(f32[5,1,8,128]{3,2,1,0:T(8,128)S(1)} %get-tuple-element.2046), channel_id=1, source_target_pairs={{2,0},{4,2},{6,4},{0,6},{3,1},{5,3},{7,5},{1,7},{10,8},{12,10},{14... | collective-permute-start | bytes 61448 | tf_op jit(solution)/shard_map/ppermute | solution.py:19
  18.0 23.6 %while.45 = (s32[]{:T(128)}, f32[3,3,8,32]{3,2,1,0:T(8,128)S(1)}, f32[5,5,10,32]{3,2,1,0:T(8,128)S(1)}, f32[5,5,10,3,32]{4,3,2,1,0:T(4,128)S(1)}, f32[3,3,8,3,32...) while((s32[]{:T(128)}, f32[3,3,8,32]{3,2,1,0:T(8,128)S(1)}, ...), condition=%wide.region_43.44_spmd.clone.clone, body=%wide.region_0.43_spmd.sunk.clone.clone.sunk | while | flops 6260617 | bytes 5239377 | solution.py:157
  18.4 3.6 %multiply_reduce_fusion.45 = (f32[3,8,32,32]{3,2,1,0:T(8,128)S(1)}, f32[3,8,32,32]{3,2,1,0:T(8,128)S(1)}, f32[3,8,32,32]{3,2,1,0:T(8,128)S(1)}, f32[3,8,32,32]{3...) fusion(f32[3,8,3,32]{3,2,1,0:T(4,128)S(1)} %get-tuple-element.2, ...), kind=kLoop, calls=%fused_computation.14.clone.1 | loop fusion | flops 2752512 | bytes 1514496 | tf_op jit(solution)/shard_map/while/body/eval_jaxpr/reduce_sum | solution.py:33
  26.3 3.6 %multiply_reduce_fusion.45 = (f32[3,8,32,32]{3,2,1,0:T(8,128)S(1)}, f32[3,8,32,32]{3,2,1,0:T(8,128)S(1)}, f32[3,8,32,32]{3,2,1,0:T(8,128)S(1)}, f32[3,8,32,32]{3...) fusion(f32[3,8,3,32]{3,2,1,0:T(4,128)S(1)} %get-tuple-element.2, ...), kind=kLoop, calls=%fused_computation.14.clone.1 | loop fusion | flops 2752512 | bytes 1514496 | tf_op jit(solution)/shard_map/while/body/eval_jaxpr/reduce_sum | solution.py:33
  34.2 3.6 %multiply_reduce_fusion.45 = (f32[3,8,32,32]{3,2,1,0:T(8,128)S(1)}, f32[3,8,32,32]{3,2,1,0:T(8,128)S(1)}, f32[3,8,32,32]{3,2,1,0:T(8,128)S(1)}, f32[3,8,32,32]{3...) fusion(f32[3,8,3,32]{3,2,1,0:T(4,128)S(1)} %get-tuple-element.2, ...), kind=kLoop, calls=%fused_computation.14.clone.1 | loop fusion | flops 2752512 | bytes 1514496 | tf_op jit(solution)/shard_map/while/body/eval_jaxpr/reduce_sum | solution.py:33
  42.2 2.4 %collective-permute-start.6 = (f32[1,3,8,224]{3,2,1,0:T(8,128)S(1)}, f32[1,3,8,224]{3,2,1,0:T(8,128)S(1)}, u32[]{:S(2)}, u32[]{:S(2)}) collective-permute-start(f32[1,3,8,224]{3,2,1,0:T(8,128)S(1)} %get-tuple-element.2060), channel_id=1, source_target_pairs={{0,8},{8,16},{16,24},{24,0},{1,9},{9,17},{17,25},{25,1},{2,10},{10... | collective-permute-start | bytes 64520 | tf_op jit(solution)/shard_map/ppermute | solution.py:18
  49.9 2.5 %collective-permute-start.9 = (f32[5,1,8,224]{3,2,1,0:T(8,128)S(1)}, f32[5,1,8,224]{3,2,1,0:T(8,128)S(1)}, u32[]{:S(2)}, u32[]{:S(2)}) collective-permute-start(f32[5,1,8,224]{3,2,1,0:T(8,128)S(1)} %get-tuple-element.2038), channel_id=1, source_target_pairs={{2,0},{4,2},{6,4},{0,6},{3,1},{5,3},{7,5},{1,7},{10,8},{12,10},{14... | collective-permute-start | bytes 107528 | tf_op jit(solution)/shard_map/ppermute | solution.py:19
  63.1 2.8 %collective-permute-start.15 = (f32[5,1,8,32]{3,2,1,0:T(8,128)S(1)}, f32[5,1,8,32]{3,2,1,0:T(8,128)S(1)}, u32[]{:S(2)}, u32[]{:S(2)}) collective-permute-start(f32[5,1,8,32]{3,2,1,0:T(8,128)S(1)} %get-tuple-element.2069), channel_id=1, source_target_pairs={{2,0},{4,2},{6,4},{0,6},{3,1},{5,3},{7,5},{1,7},{10,8},{12,10},{14... | collective-permute-start | bytes 15368 | tf_op jit(solution)/shard_map/ppermute | solution.py:19
  69.4 63.5 %while.46 = (s32[]{:T(128)}, f32[3,3,8,3,32]{4,3,2,1,0:T(4,128)S(1)}, f32[3,3,8,32]{3,2,1,0:T(8,128)S(1)}, f32[5,5,10,4,32]{4,3,2,1,0:T(4,128)S(1)}, f32[3,3,8,3...) while((s32[]{:T(128)}, ...), condition=%wide.region_115.116_spmd.clone.clone.clone, body=%wide.region_44.115_spmd.sunk.clone.clone.clone.sunk | while | flops 19310856 | bytes 13459565 | solution.py:212
  71.2 4.0 %fusion.356 = (f32[3,8,3,32]{3,2,1,0:T(4,128)S(1)}, f32[3,8,3,32]{3,2,1,0:T(4,128)S(1)}, f32[3,8,32,32]{3,2,1,0:T(8,128)S(1)}, f32[3,8,32,32]{3,2,1,0:T(8,128)S(...) fusion(f32[3,8,32,32]{3,2,1,0:T(8,128)S(1)} %get-tuple-element., ...), kind=kLoop, calls=%fused_computation.179.clone.1 | loop fusion | flops 2939904 | bytes 1551360 | tf_op jit(solution)/shard_map/while/body/eval_jaxpr/reduce_sum | solution.py:199
  77.1 3.1 %fusion.361 = (f32[3,8,32]{2,1,0:T(8,128)S(1)}, f32[3,8,32]{2,1,0:T(8,128)S(1)}, f32[3,8,32]{2,1,0:T(8,128)S(1)}, f32[3,8,32]{2,1,0:T(8,128)S(1)}, f32[3,8,32]{2...) fusion(f32[3,8,32,32]{3,2,1,0:T(8,128)S(1)} %get-tuple-element., ...), kind=kLoop, calls=%fused_computation.329.clone.1 | loop fusion | flops 3947520 | bytes 1158144 | tf_op jit(solution)/shard_map/while/body/eval_jaxpr/reduce_sum | solution.py:199
  82.9 4.2 %fusion.362 = (f32[3,8,3,32]{3,2,1,0:T(4,128)S(1)}, f32[3,8,3,32]{3,2,1,0:T(4,128)S(1)}, f32[3,8,3,32]{3,2,1,0:T(4,128)S(1)}, f32[3,8,3,32]{3,2,1,0:T(4,128)S(1)...) fusion(f32[3,8,32,32]{3,2,1,0:T(8,128)S(1)} %get-tuple-element., ...), kind=kLoop, calls=%fused_computation.177.clone.1 | loop fusion | flops 2612736 | bytes 1142784 | tf_op jit(solution)/shard_map/while/body/eval_jaxpr/reduce_sum | solution.py:199
  87.9 2.1 %fusion.363 = (f32[3,8,3,32]{3,2,1,0:T(4,128)S(1)}, f32[3,8,3,32]{3,2,1,0:T(4,128)S(1)}, f32[3,8,3,32]{3,2,1,0:T(4,128)S(1)}, f32[3,8,3,32]{3,2,1,0:T(4,128)S(1)...) fusion(f32[3,8,32,32]{3,2,1,0:T(8,128)S(1)} %get-tuple-element.2567, ...), kind=kLoop, calls=%fused_computation.175.clone.1 | loop fusion | flops 870912 | bytes 387072 | tf_op jit(solution)/shard_map/while/body/eval_jaxpr/reduce_sum | solution.py:199
  92.3 4.0 %fusion.356 = (f32[3,8,3,32]{3,2,1,0:T(4,128)S(1)}, f32[3,8,3,32]{3,2,1,0:T(4,128)S(1)}, f32[3,8,32,32]{3,2,1,0:T(8,128)S(1)}, f32[3,8,32,32]{3,2,1,0:T(8,128)S(...) fusion(f32[3,8,32,32]{3,2,1,0:T(8,128)S(1)} %get-tuple-element., ...), kind=kLoop, calls=%fused_computation.179.clone.1 | loop fusion | flops 2939904 | bytes 1551360 | tf_op jit(solution)/shard_map/while/body/eval_jaxpr/reduce_sum | solution.py:199
  98.3 3.1 %fusion.361 = (f32[3,8,32]{2,1,0:T(8,128)S(1)}, f32[3,8,32]{2,1,0:T(8,128)S(1)}, f32[3,8,32]{2,1,0:T(8,128)S(1)}, f32[3,8,32]{2,1,0:T(8,128)S(1)}, f32[3,8,32]{2...) fusion(f32[3,8,32,32]{3,2,1,0:T(8,128)S(1)} %get-tuple-element., ...), kind=kLoop, calls=%fused_computation.329.clone.1 | loop fusion | flops 3947520 | bytes 1158144 | tf_op jit(solution)/shard_map/while/body/eval_jaxpr/reduce_sum | solution.py:199
  104.1 4.2 %fusion.362 = (f32[3,8,3,32]{3,2,1,0:T(4,128)S(1)}, f32[3,8,3,32]{3,2,1,0:T(4,128)S(1)}, f32[3,8,3,32]{3,2,1,0:T(4,128)S(1)}, f32[3,8,3,32]{3,2,1,0:T(4,128)S(1)...) fusion(f32[3,8,32,32]{3,2,1,0:T(8,128)S(1)} %get-tuple-element., ...), kind=kLoop, calls=%fused_computation.177.clone.1 | loop fusion | flops 2612736 | bytes 1142784 | tf_op jit(solution)/shard_map/while/body/eval_jaxpr/reduce_sum | solution.py:199
  109.1 2.1 %fusion.363 = (f32[3,8,3,32]{3,2,1,0:T(4,128)S(1)}, f32[3,8,3,32]{3,2,1,0:T(4,128)S(1)}, f32[3,8,3,32]{3,2,1,0:T(4,128)S(1)}, f32[3,8,3,32]{3,2,1,0:T(4,128)S(1)...) fusion(f32[3,8,32,32]{3,2,1,0:T(8,128)S(1)} %get-tuple-element.2567, ...), kind=kLoop, calls=%fused_computation.175.clone.1 | loop fusion | flops 870912 | bytes 387072 | tf_op jit(solution)/shard_map/while/body/eval_jaxpr/reduce_sum | solution.py:199
  113.5 4.0 %fusion.356 = (f32[3,8,3,32]{3,2,1,0:T(4,128)S(1)}, f32[3,8,3,32]{3,2,1,0:T(4,128)S(1)}, f32[3,8,32,32]{3,2,1,0:T(8,128)S(1)}, f32[3,8,32,32]{3,2,1,0:T(8,128)S(...) fusion(f32[3,8,32,32]{3,2,1,0:T(8,128)S(1)} %get-tuple-element., ...), kind=kLoop, calls=%fused_computation.179.clone.1 | loop fusion | flops 2939904 | bytes 1551360 | tf_op jit(solution)/shard_map/while/body/eval_jaxpr/reduce_sum | solution.py:199
  119.4 3.1 %fusion.361 = (f32[3,8,32]{2,1,0:T(8,128)S(1)}, f32[3,8,32]{2,1,0:T(8,128)S(1)}, f32[3,8,32]{2,1,0:T(8,128)S(1)}, f32[3,8,32]{2,1,0:T(8,128)S(1)}, f32[3,8,32]{2...) fusion(f32[3,8,32,32]{3,2,1,0:T(8,128)S(1)} %get-tuple-element., ...), kind=kLoop, calls=%fused_computation.329.clone.1 | loop fusion | flops 3947520 | bytes 1158144 | tf_op jit(solution)/shard_map/while/body/eval_jaxpr/reduce_sum | solution.py:199
  125.2 4.2 %fusion.362 = (f32[3,8,3,32]{3,2,1,0:T(4,128)S(1)}, f32[3,8,3,32]{3,2,1,0:T(4,128)S(1)}, f32[3,8,3,32]{3,2,1,0:T(4,128)S(1)}, f32[3,8,3,32]{3,2,1,0:T(4,128)S(1)...) fusion(f32[3,8,32,32]{3,2,1,0:T(8,128)S(1)} %get-tuple-element., ...), kind=kLoop, calls=%fused_computation.177.clone.1 | loop fusion | flops 2612736 | bytes 1142784 | tf_op jit(solution)/shard_map/while/body/eval_jaxpr/reduce_sum | solution.py:199
  137.4 3.0 %collective-permute-done.18 = f32[1,3,8,896]{3,2,1,0:T(8,128)S(1)} collective-permute-done((f32[1,3,8,896]{3,2,1,0:T(8,128)S(1)}, f32[1,3,8,896]{3,2,1,0:T(8,128)S(1)}, u32[]{:S(2)}, u32[]{:S(2)}) %collective-permute-start.18) | collective-permute-done | bytes 86048 | tf_op jit(solution)/shard_map/ppermute | solution.py:18
  141.8 2.7 %collective-permute-start.21 = (f32[5,1,8,896]{3,2,1,0:T(8,128)S(1)}, f32[5,1,8,896]{3,2,1,0:T(8,128)S(1)}, u32[]{:S(2)}, u32[]{:S(2)}) collective-permute-start(f32[5,1,8,896]{3,2,1,0:T(8,128)S(1)} %get-tuple-element.1993), channel_id=1, source_target_pairs={{2,0},{4,2},{6,4},{0,6},{3,1},{5,3},{7,5},{1,7},{10,8},{12,10},{14... | collective-permute-start | bytes 430088 | tf_op jit(solution)/shard_map/ppermute | solution.py:19
  144.6 4.6 %collective-permute-done.20 = f32[5,1,8,896]{3,2,1,0:T(8,128)S(1)} collective-permute-done((f32[5,1,8,896]{3,2,1,0:T(8,128)S(1)}, f32[5,1,8,896]{3,2,1,0:T(8,128)S(1)}, u32[]{:S(2)}, u32[]{:S(2)}) %collective-permute-start.20) | collective-permute-done | bytes 143392 | tf_op jit(solution)/shard_map/ppermute | solution.py:18
  (465 shorter events, 77.7 us)
Async XLA Ops:
  1.6 5.6 %collective-permute-start = (f32[1,3,8,128]{3,2,1,0:T(8,128)S(1)}, f32[1,3,8,128]{3,2,1,0:T(8,128)S(1)}, u32[]{:S(2)}, u32[]{:S(2)}) collective-permute-start(f32[1,3,8,128]{3,2,1,0:T(8,128)S(1)} %get-tuple-element.2066), channel_id=1, source_target_pairs={{0,8},{8,16},{16,24},{24,0},{1,9},{9,17},{17,25},{25,1},{2,10},{10... | collective-permute-start | bytes 36872 | tf_op jit(solution)/shard_map/ppermute | solution.py:18
  4.6 3.7 %collective-permute-start.1 = (f32[1,3,8,128]{3,2,1,0:T(8,128)S(1)}, f32[1,3,8,128]{3,2,1,0:T(8,128)S(1)}, u32[]{:S(2)}, u32[]{:S(2)}) collective-permute-start(f32[1,3,8,128]{3,2,1,0:T(8,128)S(1)} %get-tuple-element.2067), channel_id=1, source_target_pairs={{8,0},{16,8},{24,16},{0,24},{9,1},{17,9},{25,17},{1,25},{10,2},{18... | collective-permute-start | bytes 36872 | tf_op jit(solution)/shard_map/ppermute | solution.py:19
  9.1 5.6 %collective-permute-start.2 = (f32[5,1,8,128]{3,2,1,0:T(8,128)S(1)}, f32[5,1,8,128]{3,2,1,0:T(8,128)S(1)}, u32[]{:S(2)}, u32[]{:S(2)}) collective-permute-start(f32[5,1,8,128]{3,2,1,0:T(8,128)S(1)} %get-tuple-element.2045), channel_id=1, source_target_pairs={{0,2},{2,4},{4,6},{6,0},{1,3},{3,5},{5,7},{7,1},{8,10},{10,12},{12... | collective-permute-start | bytes 61448 | tf_op jit(solution)/shard_map/ppermute | solution.py:18
  10.6 4.0 %collective-permute-start.3 = (f32[5,1,8,128]{3,2,1,0:T(8,128)S(1)}, f32[5,1,8,128]{3,2,1,0:T(8,128)S(1)}, u32[]{:S(2)}, u32[]{:S(2)}) collective-permute-start(f32[5,1,8,128]{3,2,1,0:T(8,128)S(1)} %get-tuple-element.2046), channel_id=1, source_target_pairs={{2,0},{4,2},{6,4},{0,6},{3,1},{5,3},{7,5},{1,7},{10,8},{12,10},{14... | collective-permute-start | bytes 61448 | tf_op jit(solution)/shard_map/ppermute | solution.py:19
  15.6 1.2 collective-permute-start.4
  15.7 1.3 collective-permute-start.5
  42.2 4.8 %collective-permute-start.6 = (f32[1,3,8,224]{3,2,1,0:T(8,128)S(1)}, f32[1,3,8,224]{3,2,1,0:T(8,128)S(1)}, u32[]{:S(2)}, u32[]{:S(2)}) collective-permute-start(f32[1,3,8,224]{3,2,1,0:T(8,128)S(1)} %get-tuple-element.2060), channel_id=1, source_target_pairs={{0,8},{8,16},{16,24},{24,0},{1,9},{9,17},{17,25},{25,1},{2,10},{10... | collective-permute-start | bytes 64520 | tf_op jit(solution)/shard_map/ppermute | solution.py:18
  44.7 3.8 %collective-permute-start.7 = (f32[1,3,8,224]{3,2,1,0:T(8,128)S(1)}, f32[1,3,8,224]{3,2,1,0:T(8,128)S(1)}, u32[]{:S(2)}, u32[]{:S(2)}) collective-permute-start(f32[1,3,8,224]{3,2,1,0:T(8,128)S(1)} %get-tuple-element.2061), channel_id=1, source_target_pairs={{8,0},{16,8},{24,16},{0,24},{9,1},{17,9},{25,17},{1,25},{10,2},{18... | collective-permute-start | bytes 64520 | tf_op jit(solution)/shard_map/ppermute | solution.py:19
  48.5 6.0 %collective-permute-start.8 = (f32[5,1,8,224]{3,2,1,0:T(8,128)S(1)}, f32[5,1,8,224]{3,2,1,0:T(8,128)S(1)}, u32[]{:S(2)}, u32[]{:S(2)}) collective-permute-start(f32[5,1,8,224]{3,2,1,0:T(8,128)S(1)} %get-tuple-element.2037), channel_id=1, source_target_pairs={{0,2},{2,4},{4,6},{6,0},{1,3},{3,5},{5,7},{7,1},{8,10},{10,12},{12... | collective-permute-start | bytes 107528 | tf_op jit(solution)/shard_map/ppermute | solution.py:18
  49.9 4.6 %collective-permute-start.9 = (f32[5,1,8,224]{3,2,1,0:T(8,128)S(1)}, f32[5,1,8,224]{3,2,1,0:T(8,128)S(1)}, u32[]{:S(2)}, u32[]{:S(2)}) collective-permute-start(f32[5,1,8,224]{3,2,1,0:T(8,128)S(1)} %get-tuple-element.2038), channel_id=1, source_target_pairs={{2,0},{4,2},{6,4},{0,6},{3,1},{5,3},{7,5},{1,7},{10,8},{12,10},{14... | collective-permute-start | bytes 107528 | tf_op jit(solution)/shard_map/ppermute | solution.py:19
  54.5 1.3 collective-permute-start.10
  54.6 1.3 collective-permute-start.11
  56.8 4.6 %collective-permute-start.12 = (f32[1,3,8,32]{3,2,1,0:T(8,128)S(1)}, f32[1,3,8,32]{3,2,1,0:T(8,128)S(1)}, u32[]{:S(2)}, u32[]{:S(2)}) collective-permute-start(f32[1,3,8,32]{3,2,1,0:T(8,128)S(1)} %get-tuple-element.2070), channel_id=1, source_target_pairs={{0,8},{8,16},{16,24},{24,0},{1,9},{9,17},{17,25},{25,1},{2,10},{10... | collective-permute-start | bytes 9224 | tf_op jit(solution)/shard_map/ppermute | solution.py:18
  58.4 3.7 %collective-permute-start.13 = (f32[1,3,8,32]{3,2,1,0:T(8,128)S(1)}, f32[1,3,8,32]{3,2,1,0:T(8,128)S(1)}, u32[]{:S(2)}, u32[]{:S(2)}) collective-permute-start(f32[1,3,8,32]{3,2,1,0:T(8,128)S(1)} %get-tuple-element.2071), channel_id=1, source_target_pairs={{8,0},{16,8},{24,16},{0,24},{9,1},{17,9},{25,17},{1,25},{10,2},{18... | collective-permute-start | bytes 9224 | tf_op jit(solution)/shard_map/ppermute | solution.py:19
  62.1 5.7 %collective-permute-start.14 = (f32[5,1,8,32]{3,2,1,0:T(8,128)S(1)}, f32[5,1,8,32]{3,2,1,0:T(8,128)S(1)}, u32[]{:S(2)}, u32[]{:S(2)}) collective-permute-start(f32[5,1,8,32]{3,2,1,0:T(8,128)S(1)} %get-tuple-element.2068), channel_id=1, source_target_pairs={{0,2},{2,4},{4,6},{6,0},{1,3},{3,5},{5,7},{7,1},{8,10},{10,12},{12... | collective-permute-start | bytes 15368 | tf_op jit(solution)/shard_map/ppermute | solution.py:18
  63.1 4.7 %collective-permute-start.15 = (f32[5,1,8,32]{3,2,1,0:T(8,128)S(1)}, f32[5,1,8,32]{3,2,1,0:T(8,128)S(1)}, u32[]{:S(2)}, u32[]{:S(2)}) collective-permute-start(f32[5,1,8,32]{3,2,1,0:T(8,128)S(1)} %get-tuple-element.2069), channel_id=1, source_target_pairs={{2,0},{4,2},{6,4},{0,6},{3,1},{5,3},{7,5},{1,7},{10,8},{12,10},{14... | collective-permute-start | bytes 15368 | tf_op jit(solution)/shard_map/ppermute | solution.py:19
  67.8 1.2 collective-permute-start.16
  67.9 1.3 collective-permute-start.17
  134.0 6.4 %collective-permute-start.18 = (f32[1,3,8,896]{3,2,1,0:T(8,128)S(1)}, f32[1,3,8,896]{3,2,1,0:T(8,128)S(1)}, u32[]{:S(2)}, u32[]{:S(2)}) collective-permute-start(f32[1,3,8,896]{3,2,1,0:T(8,128)S(1)} %get-tuple-element.2002), channel_id=1, source_target_pairs={{0,8},{8,16},{16,24},{24,0},{1,9},{9,17},{17,25},{25,1},{2,10},{10... | collective-permute-start | bytes 258056 | tf_op jit(solution)/shard_map/ppermute | solution.py:18
  135.2 5.5 %collective-permute-start.19 = (f32[1,3,8,896]{3,2,1,0:T(8,128)S(1)}, f32[1,3,8,896]{3,2,1,0:T(8,128)S(1)}, u32[]{:S(2)}, u32[]{:S(2)}) collective-permute-start(f32[1,3,8,896]{3,2,1,0:T(8,128)S(1)} %get-tuple-element.2003), channel_id=1, source_target_pairs={{8,0},{16,8},{24,16},{0,24},{9,1},{17,9},{25,17},{1,25},{10,2},{18... | collective-permute-start | bytes 258056 | tf_op jit(solution)/shard_map/ppermute | solution.py:19
  140.7 8.5 %collective-permute-start.20 = (f32[5,1,8,896]{3,2,1,0:T(8,128)S(1)}, f32[5,1,8,896]{3,2,1,0:T(8,128)S(1)}, u32[]{:S(2)}, u32[]{:S(2)}) collective-permute-start(f32[5,1,8,896]{3,2,1,0:T(8,128)S(1)} %get-tuple-element.1992), channel_id=1, source_target_pairs={{0,2},{2,4},{4,6},{6,0},{1,3},{3,5},{5,7},{7,1},{8,10},{10,12},{12... | collective-permute-start | bytes 430088 | tf_op jit(solution)/shard_map/ppermute | solution.py:18
  141.8 8.1 %collective-permute-start.21 = (f32[5,1,8,896]{3,2,1,0:T(8,128)S(1)}, f32[5,1,8,896]{3,2,1,0:T(8,128)S(1)}, u32[]{:S(2)}, u32[]{:S(2)}) collective-permute-start(f32[5,1,8,896]{3,2,1,0:T(8,128)S(1)} %get-tuple-element.1993), channel_id=1, source_target_pairs={{2,0},{4,2},{6,4},{0,6},{3,1},{5,3},{7,5},{1,7},{10,8},{12,10},{14... | collective-permute-start | bytes 430088 | tf_op jit(solution)/shard_map/ppermute | solution.py:19
  150.0 1.4 collective-permute-start.22
  150.1 1.4 collective-permute-start.23
  (13 other events, 24.3 us)
where the time goes:
time: 153 us
  other arithmetic  88.9 us (58%)
  starting transfers between devices  30.6 us (20%)
  waiting for transfers between devices  25.6 us (17%)
  local copies, waits for them, and re-layouts  4.73 us (3%)
  loops' own time  2.33 us (2%)
    reduce_sum x9, other arithmetic, half_force_step(): jnp.sum(pair_force, axis=-2)  30.8 us
    ppermute x12, waiting for transfers between devices, padded_2(): before = lax.ppermute(last, axis, up)  20.8 us
    ppermute x12, starting transfers between devices, padded_2(): after = lax.ppermute(first, axis, down)  17.1 us
    reduce_sum x6, other arithmetic, half_force_step(): jnp.sum(energy_pair, axis=-2)[..., None, :]  14.6 us
    ppermute x12, starting transfers between devices, padded_2(): before = lax.ppermute(last, axis, up)  13.5 us
    reduce_sum x6, other arithmetic, separation(): return (displace, jnp.sum(displace * displace, axis=-3))  12 us
    mul x9, other arithmetic, half_force_step(): pair_force = 2.0 * coupling[..., None, :, :] * displace  10.3 us
    reduce_sum x6, other arithmetic, half_density_step(): jnp.sum(dens * plane_weight[..., :, None], axis=-2)  9.75 us
  transfers between devices with their start and end apart: 24, of which 21 were waited for; matrix products, arithmetic and copies ran while one was open for 0% of the time, Pallas kernels for 0%

commit v1 on v0

v1 whole, which is shorter than its diff:
```python
import functools
import math

import jax
import jax.numpy as jnp
from jax import lax
from jax.experimental import pallas as pl
from jax.experimental.pallas import tpu as pltpu
from jax.sharding import PartitionSpec as P

cut_square = 0.9025
density_rate = 3.0
unit = density_rate * math.log2(math.e)
alpha = math.sqrt(unit)
kappa = unit * cut_square
tail = 2.0**-kappa
shift_big = 2.0 * kappa / (cut_square * density_rate)
density_scale = tail / kappa**2
energy_scale = 0.25 * tail**2 / kappa**2
force_scale = -2.0 * tail**2 * density_rate / (kappa**2 * alpha)
slope_scale = -0.5 / tail

AXES = ("gx", "gy", "gz")
DIRECTIONS = [
    (a, b, c)
    for a in (-1, 0, 1)
    for b in (-1, 0, 1)
    for c in (-1, 0, 1)
    if (a, b, c) != (0, 0, 0)
]


def kernel(dims, axis_sizes, pay_ref, out_ref, pad, pad_phi, spread, spread_phi, own, hot, block,
           pair_e, pair_m, pair_q, send_sem, recv_sem, send_phi, recv_phi):
    nx, ny, nz, slots = dims
    lanes = nz * slots
    me = [lax.axis_index(axis) for axis in AXES]

    def peer(direction):
        return {
            axis: lax.rem(place + step + size, size)
            for axis, place, step, size in zip(AXES, me, direction, axis_sizes)
        }

    barrier = pltpu.get_barrier_semaphore()
    for direction in DIRECTIONS:
        pl.semaphore_signal(
            barrier, inc=1, device_id=peer(direction), device_id_type=pl.DeviceIdType.MESH
        )
    pl.semaphore_wait(barrier, len(DIRECTIONS))

    def source_range(step, length):
        return pl.ds(length - 1, 1) if step > 0 else pl.ds(0, 1) if step < 0 else pl.ds(0, length)

    def target_range(step, length):
        return pl.ds(0, 1) if step > 0 else pl.ds(length + 1, 1) if step < 0 else pl.ds(1, length)

    copies = []
    for index, direction in enumerate(DIRECTIONS):
        a, b, c = direction
        zs = source_range(c, nz)
        copy = pltpu.make_async_remote_copy(
            src_ref=pay_ref.at[source_range(a, nx), source_range(b, ny), zs],
            dst_ref=pad.at[target_range(a, nx), target_range(b, ny), 1 - c, zs],
            send_sem=send_sem.at[index],
            recv_sem=recv_sem.at[index],
            device_id=peer(direction),
            device_id_type=pl.DeviceIdType.MESH,
        )
        copy.start()
        copies.append(copy)

    row = lax.broadcasted_iota(jnp.int32, (9 * nz, lanes), 0) % (3 * nz)
    cell = lax.broadcasted_iota(jnp.int32, (9 * nz, lanes), 1) // slots
    for dz in range(3):
        hot[:, dz * lanes : (dz + 1) * lanes] = jnp.where(
            row == cell + (nz - 1 + dz), 1.0, 0.0
        ).astype(jnp.bfloat16)
    block_row = lax.broadcasted_iota(jnp.int32, (lanes, lanes), 0) // slots
    block_col = lax.broadcasted_iota(jnp.int32, (lanes, lanes), 1) // slots
    block[...] = jnp.where(block_row == block_col, 1.0, 0.0).astype(jnp.bfloat16)
    diagonal = (
        lax.broadcasted_iota(jnp.int32, (slots, lanes), 1) % slots
        == lax.broadcasted_iota(jnp.int32, (slots, lanes), 0)
    )

    for x in range(nx):
        for y in range(ny):
            pad[x + 1, y + 1, 1] = pay_ref[x, y]

    for copy in copies:
        copy.wait()

    zrow = lax.broadcasted_iota(jnp.int32, (3 * nz, 4 * slots), 0)
    valid = (zrow >= nz - 1) & (zrow <= 2 * nz)

    def pieces(value):
        high = value.astype(jnp.bfloat16).astype(jnp.float32)
        rest = value - high
        middle = rest.astype(jnp.bfloat16).astype(jnp.float32)
        return high, middle, rest - middle

    def expand(t, carry):
        x, y = t // (ny + 2), t % (ny + 2)
        value = jnp.concatenate([pad[x, y, 0], pad[x, y, 1], pad[x, y, 2]], axis=0)
        value = jnp.where(valid, value, 0.0)
        stacked = jnp.concatenate(pieces(value), axis=0).astype(jnp.bfloat16)
        for dz in range(3):
            spread[x, y, dz] = lax.dot_general(
                stacked,
                hot[:, dz * lanes : (dz + 1) * lanes],
                (((0,), (0,)), ((), ())),
                preferred_element_type=jnp.float32,
            )
        return carry

    lax.fori_loop(0, (nx + 2) * (ny + 2), expand, 0)

    def density(t, carry):
        x, y = t // ny, t % ny
        mine = [
            jnp.sum(
                jnp.where(diagonal, spread[x + 1, y + 1, 1, k * slots : (k + 1) * slots, :], 0.0),
                axis=0,
                keepdims=True,
            )
            for k in range(4)
        ]
        for k in range(4):
            own[t, k : k + 1, :] = mine[k]

        def step(n, sums):
            rho, energy = sums
            a, b = n // 3, n % 3
            px = jnp.broadcast_to(mine[0] - (a - 1).astype(jnp.float32) * alpha, (8, lanes))
            py = jnp.broadcast_to(mine[1] - (b - 1).astype(jnp.float32) * alpha, (8, lanes))
            for dz in range(3):
                pz = jnp.broadcast_to(mine[2] - (dz - 1) * alpha, (8, lanes))
                for r in range(0, slots, 8):
                    dx = spread[x + a, y + b, dz, r : r + 8, :] - px
                    dy = spread[x + a, y + b, dz, slots + r : slots + r + 8, :] - py
                    dd = spread[x + a, y + b, dz, 2 * slots + r : 2 * slots + r + 8, :] - pz
                    wj = spread[x + a, y + b, dz, 3 * slots + r : 3 * slots + r + 8, :]
                    m = jnp.maximum(kappa - (dx * dx + dy * dy + dd * dd), 0.0)
                    e = jnp.exp2(m)
                    em = e * m
                    q = em * wj
                    rho = rho + q * m
                    energy = energy + q * em
                    pair_e[t, n, dz, r : r + 8, :] = e
                    pair_m[t, n, dz, r : r + 8, :] = m
                    pair_q[t, n, dz, r : r + 8, :] = q
            return rho, energy

        zero = jnp.zeros((8, lanes), jnp.float32)
        rho, energy = lax.fori_loop(0, 9, step, (zero, zero))
        w = mine[3]
        rho = jnp.sum(rho, axis=0, keepdims=True) * density_scale - w
        energy = jnp.sum(energy, axis=0, keepdims=True) * (energy_scale * w) - 0.25 * w * w
        root = jnp.sqrt(jnp.maximum(rho, 0.0) + 1.0)
        big = w > 1.3
        ratio = jnp.where(big, 0.875, jnp.where(w > 0.5, 1.0, 0.0))
        a = jnp.where(big, 1.4, jnp.where(w > 0.5, 1.0, 0.0))
        phi = slope_scale * ratio / root
        out_ref[t, 3:4, :] = energy - a * root
        pad_phi[x + 1, y + 1, :, 128 : 128 + lanes] = phi
        return carry

    lax.fori_loop(0, nx * ny, density, 0)

    def lane_source(step):
        return (
            pl.ds(lanes, 128) if step > 0 else pl.ds(128, 128) if step < 0 else pl.ds(128, lanes)
        )

    def lane_target(step):
        return (
            pl.ds(0, 128)
            if step > 0
            else pl.ds(128 + lanes, 128)
            if step < 0
            else pl.ds(128, lanes)
        )

    def inner_source(step, length):
        return pl.ds(length, 1) if step > 0 else pl.ds(1, 1) if step < 0 else pl.ds(1, length)

    copies = []
    for index, direction in enumerate(DIRECTIONS):
        a, b, c = direction
        copy = pltpu.make_async_remote_copy(
            src_ref=pad_phi.at[inner_source(a, nx), inner_source(b, ny), :, lane_source(c)],
            dst_ref=pad_phi.at[target_range(a, nx), target_range(b, ny), :, lane_target(c)],
            send_sem=send_phi.at[index],
            recv_sem=recv_phi.at[index],
            device_id=peer(direction),
            device_id_type=pl.DeviceIdType.MESH,
        )
        copy.start()
        copies.append(copy)
    for copy in copies:
        copy.wait()

    def expand_phi(t, carry):
        x, y = t // (ny + 2), t % (ny + 2)
        value = pad_phi[x, y]
        for dz in range(3):
            start = 128 + (dz - 1) * slots
            part = jnp.where(diagonal, value[:, start : start + lanes], 0.0)
            stacked = jnp.concatenate(pieces(part), axis=0).astype(jnp.bfloat16)
            result = jnp.dot(stacked, block[...], preferred_element_type=jnp.float32)
            spread_phi[x, y, dz] = (
                result[:slots] + result[slots : 2 * slots] + result[2 * slots :]
            )
        return carry

    lax.fori_loop(0, (nx + 2) * (ny + 2), expand_phi, 0)

    def force(t, carry):
        x, y = t // ny, t % ny
        mine = [own[t, k : k + 1, :] for k in range(4)]
        phi = jnp.broadcast_to(pad_phi[x + 1, y + 1, :, 128 : 128 + lanes], (8, lanes))

        def step(n, sums):
            fx, fy, fz = sums
            a, b = n // 3, n % 3
            px = jnp.broadcast_to(mine[0] - (a - 1).astype(jnp.float32) * alpha, (8, lanes))
            py = jnp.broadcast_to(mine[1] - (b - 1).astype(jnp.float32) * alpha, (8, lanes))
            for dz in range(3):
                pz = jnp.broadcast_to(mine[2] - (dz - 1) * alpha, (8, lanes))
                for r in range(0, slots, 8):
                    dx = spread[x + a, y + b, dz, r : r + 8, :] - px
                    dy = spread[x + a, y + b, dz, slots + r : slots + r + 8, :] - py
                    dd = spread[x + a, y + b, dz, 2 * slots + r : 2 * slots + r + 8, :] - pz
                    e = pair_e[t, n, dz, r : r + 8, :]
                    m = pair_m[t, n, dz, r : r + 8, :]
                    q = pair_q[t, n, dz, r : r + 8, :]
                    both = phi + spread_phi[x + a, y + b, dz, r : r + 8, :]
                    v = q * (both * (m + shift_big) + e * (m + 0.5 * shift_big))
                    fx = fx + v * dx
                    fy = fy + v * dy
                    fz = fz + v * dd
            return fx, fy, fz

        zero = jnp.zeros((8, lanes), jnp.float32)
        sums = lax.fori_loop(0, 9, step, (zero, zero, zero))
        scale = force_scale * mine[3]
        for k in range(3):
            out_ref[t, k : k + 1, :] = jnp.sum(sums[k], axis=0, keepdims=True) * scale
        return carry

    lax.fori_loop(0, nx * ny, force, 0)


def body(axis_sizes, positions, types):
    nx, ny, nz, slots = types.shape
    lanes = nz * slots
    weight = jnp.where(types == 1, 1.0, jnp.where(types == 2, 1.6, 0.0)).astype(jnp.float32)
    payload = jnp.concatenate([positions * alpha, weight], axis=3)
    count = len(DIRECTIONS)
    columns = nx * ny
    out = pl.pallas_call(
        functools.partial(kernel, (nx, ny, nz, slots), axis_sizes),
        out_shape=jax.ShapeDtypeStruct((columns, 4, lanes), jnp.float32),
        in_specs=[pl.BlockSpec(memory_space=pltpu.VMEM)],
        out_specs=pl.BlockSpec(memory_space=pltpu.VMEM),
        scratch_shapes=[
            pltpu.VMEM((nx + 2, ny + 2, 3, nz, 4 * slots), jnp.float32),
            pltpu.VMEM((nx + 2, ny + 2, 1, lanes + 256), jnp.float32),
            pltpu.VMEM((nx + 2, ny + 2, 3, 4 * slots, lanes), jnp.float32),
            pltpu.VMEM((nx + 2, ny + 2, 3, slots, lanes), jnp.float32),
            pltpu.VMEM((columns, 8, lanes), jnp.float32),
            pltpu.VMEM((9 * nz, 3 * lanes), jnp.bfloat16),
            pltpu.VMEM((lanes, lanes), jnp.bfloat16),
            pltpu.VMEM((columns, 9, 3, slots, lanes), jnp.float32),
            pltpu.VMEM((columns, 9, 3, slots, lanes), jnp.float32),
            pltpu.VMEM((columns, 9, 3, slots, lanes), jnp.float32),
            pltpu.SemaphoreType.DMA((count,)),
            pltpu.SemaphoreType.DMA((count,)),
            pltpu.SemaphoreType.DMA((count,)),
            pltpu.SemaphoreType.DMA((count,)),
        ],
        compiler_params=pltpu.CompilerParams(
            collective_id=0, has_side_effects=True, vmem_limit_bytes=60 * 1024 * 1024
        ),
    )(payload)
    out = out.reshape(nx, ny, 4, nz, slots).transpose(0, 1, 3, 2, 4)
    return out.reshape(nx, ny, nz, 4 * slots)


def solution(mesh):
    spec = P("gx", "gy", "gz", None)
    sizes = tuple(mesh.shape[axis] for axis in AXES)
    return jax.shard_map(
        functools.partial(body, sizes),
        mesh=mesh,
        in_specs=(spec, spec),
        out_specs=spec,
        check_vma=False,
    )
```

time: 153 us -> 47.5 us (0.31)
  other arithmetic: 88.9 us -> 1.49 us
  Pallas kernels: 0 us -> 44 us
  starting transfers between devices: 30.6 us -> 0 us
  waiting for transfers between devices: 25.6 us -> 0 us
  local copies, waits for them, and re-layouts: 4.73 us -> 1.65 us
  loops' own time: 2.33 us -> 0 us
    reduce_sum x27 -> x0, other arithmetic: 67.1 us -> none  [the longest x9 30.8 us: half_force_step(): jnp.sum(pair_force, axis=-2)]
    pallas_call x0 -> x1, Pallas kernels: none -> 44 us  [body(): pl.pallas_call(functools.partial(kernel, (nx, ny, nz, slots), axis_sizes)...]
    ppermute x24 -> x0, starting transfers between devices: 30.6 us -> none  [the longest x12 17.1 us: padded_2(): after = lax.ppermute(first, axis, down)]
    ppermute x24 -> x0, waiting for transfers between devices: 25.6 us -> none  [the longest x12 20.8 us: padded_2(): before = lax.ppermute(last, axis, up)]
    mul x9 -> x1, other arithmetic: 10.3 us -> 0.78 us  [body(): payload = jnp.concatenate([positions * alpha, weight], axis=3)]
    dynamic_update_slice x93 -> x0, other arithmetic: 3.38 us -> none  [put_row(): return lax.dynamic_update_index_in_dim(array, value, index, 0)]
    slice x15 -> x0, other arithmetic: 3.16 us -> none  [the longest x9 2.76 us: padded_2(): last = lax.slice_in_dim(value, length - width, length, axis=dim)]
    another operation x2 -> x0, loops' own time: 2.33 us -> none  [the longest x1 1.39 us: body(): lax.fori_loop(0, cell_count_first, half_force_step, (force_start, pair_st...]
  transfers between devices with their start and end apart: 24 -> 0, of which waited for: 21 -> 0; matrix products, arithmetic and copies ran while one was open for 0% -> 0% of each run, Pallas kernels for 0% -> 0%
where the time goes in v1:
time: 47.5 us; the launch traced here: 47.2 us
  Pallas kernels  44 us (93%)
  local copies, waits for them, and re-layouts  1.65 us (3%)
  other arithmetic  1.49 us (3%)
    pallas_call x1, Pallas kernels, body(): pl.pallas_call(functools.partial(kernel, (nx, ny, nz, slots), axis_sizes)...  44 us

profile of v1, /device:TPU:0, one launch (start us, length us, event | category | flops | bytes accessed | tf_op | source)
XLA Modules:
  0.0 47.2 jit_solution(15573361176364283768)
XLA Ops:
  0.0 0.0 copy-start
  0.0 0.8 %broadcast_multiply_fusion = f32[3,3,8,96]{3,2,1,0:T(8,128)S(1)} fusion(f32[3,3,8,96]{3,2,1,0:T(8,128)} %param.2), kind=kLoop, calls=%fused_computation.2 | loop fusion | flops 6912 | bytes 55296 | tf_op jit(solution)/shard_map/mul | solution.py:259
  0.8 0.0 copy-done
  0.8 0.7 %pad_maximum_fusion.pay_ref = f32[3,3,8,128]{3,2,1,0:T(8,128)} fusion(f32[3,3,8,32]{3,2,1,0:T(8,128)S(1)} %select_select_fusion, f32[3,3,8,96]{3,2,1,0:T(8,128)S(1)} %broadcast_multiply_fusion), kind=kLoop, calls=%fused_computation | loop fusion | flops 9216 | bytes 73728 | tf_op jit(solution)/shard_map/concatenate | solution.py:259
  1.5 44.0 %shard_map.28 = f32[9,4,256]{2,1,0:T(4,128)} custom-call(f32[3,3,8,128]{3,2,1,0:T(8,128)} %pad_maximum_fusion.pay_ref), custom_call_target="tpu_custom_call" | custom-call | tf_op jit(solution)/shard_map/pallas_call | solution.py:262
  45.6 0.9 %reshape.6 = f32[3,3,4,8,32]{4,3,2,1,0:T(8,128)S(1)} reshape(f32[9,4,256]{2,1,0:T(4,128)} %shard_map.28) | data formatting | bytes 73728 | tf_op jit(solution)/shard_map/reshape | solution.py:287
  46.5 0.7 %reshape.7 = f32[3,3,8,128]{3,2,1,0:T(8,128)} reshape(f32[3,3,8,4,32]{4,3,2,1,0:T(4,128)S(1)} %copy.3) | data formatting | bytes 73728 | tf_op jit(solution)/shard_map/reshape | solution.py:288
  (2 shorter events, 0.0 us)
Async XLA Ops:
  0.0 0.8 %copy-start = (s32[3,3,8,32]{3,2,1,0:T(8,128)S(1)}, s32[3,3,8,32]{3,2,1,0:T(8,128)}, u32[]{:S(2)}) copy-start(s32[3,3,8,32]{3,2,1,0:T(8,128)} %param.3) | copy-start | bytes 27652

commit v2 on v1

--- a/solution.py
+++ b/solution.py
@@ -26,7 +26,7 @@
     for a in (-1, 0, 1)
     for b in (-1, 0, 1)
     for c in (-1, 0, 1)
-    if (a, b, c) != (0, 0, 0)
+    if (c != 0) != ((a, b) != (0, 0))
 ]
 
 
@@ -55,20 +55,58 @@
     def target_range(step, length):
         return pl.ds(0, 1) if step > 0 else pl.ds(length + 1, 1) if step < 0 else pl.ds(1, length)
 
+    def column_source(step, length):
+        return pl.ds(length, 1) if step > 0 else pl.ds(1, 1) if step < 0 else pl.ds(1, length)
+
+    def send(index, source, target, send_sems, recv_sems):
+        copy = pltpu.make_async_remote_copy(
+            src_ref=source,
+            dst_ref=target,
+            send_sem=send_sems.at[index],
+            recv_sem=recv_sems.at[index],
+            device_id=peer(DIRECTIONS[index]),
+            device_id_type=pl.DeviceIdType.MESH,
+        )
+        copy.start()
+        return copy
+
+    along = [k for k, d in enumerate(DIRECTIONS) if d[2] != 0]
+    across = [k for k, d in enumerate(DIRECTIONS) if d[2] == 0]
+
+    def send_across(array, send_sems, recv_sems):
+        copies = []
+        for k in across:
+            a, b, _ = DIRECTIONS[k]
+            copies.append(
+                send(
+                    k,
+                    array.at[column_source(a, nx), column_source(b, ny)],
+                    array.at[target_range(a, nx), target_range(b, ny)],
+                    send_sems,
+                    recv_sems,
+                )
+            )
+        return copies
+
     copies = []
-    for index, direction in enumerate(DIRECTIONS):
-        a, b, c = direction
+    for k in along:
+        c = DIRECTIONS[k][2]
         zs = source_range(c, nz)
-        copy = pltpu.make_async_remote_copy(
-            src_ref=pay_ref.at[source_range(a, nx), source_range(b, ny), zs],
-            dst_ref=pad.at[target_range(a, nx), target_range(b, ny), 1 - c, zs],
-            send_sem=send_sem.at[index],
-            recv_sem=recv_sem.at[index],
-            device_id=peer(direction),
-            device_id_type=pl.DeviceIdType.MESH,
-        )
-        copy.start()
-        copies.append(copy)
+        copies.append(
+            send(
+                k,
+                pay_ref.at[:, :, zs],
+                pad.at[pl.ds(1, nx), pl.ds(1, ny), 1 - c, zs],
+                send_sem,
+                recv_sem,
+            )
+        )
+    for x in range(nx):
+        for y in range(ny):
+            pad[x + 1, y + 1, 1] = pay_ref[x, y]
+    for copy in copies:
+        copy.wait()
+    copies = send_across(pad, send_sem, recv_sem)
 
     row = lax.broadcasted_iota(jnp.int32, (9 * nz, lanes), 0) % (3 * nz)
     cell = lax.broadcasted_iota(jnp.int32, (9 * nz, lanes), 1) // slots
@@ -83,10 +121,6 @@
         lax.broadcasted_iota(jnp.int32, (slots, lanes), 1) % slots
         == lax.broadcasted_iota(jnp.int32, (slots, lanes), 0)
     )
-
-    for x in range(nx):
-        for y in range(ny):
-            pad[x + 1, y + 1, 1] = pay_ref[x, y]
 
     for copy in copies:
         copy.wait()
@@ -182,23 +216,21 @@
             else pl.ds(128, lanes)
         )
 
-    def inner_source(step, length):
-        return pl.ds(length, 1) if step > 0 else pl.ds(1, 1) if step < 0 else pl.ds(1, length)
-
     copies = []
-    for index, direction in enumerate(DIRECTIONS):
-        a, b, c = direction
-        copy = pltpu.make_async_remote_copy(
-            src_ref=pad_phi.at[inner_source(a, nx), inner_source(b, ny), :, lane_source(c)],
-            dst_ref=pad_phi.at[target_range(a, nx), target_range(b, ny), :, lane_target(c)],
-            send_sem=send_phi.at[index],
-            recv_sem=recv_phi.at[index],
-            device_id=peer(direction),
-            device_id_type=pl.DeviceIdType.MESH,
-        )
-        copy.start()
-        copies.append(copy)
+    for k in along:
+        c = DIRECTIONS[k][2]
+        copies.append(
+            send(
+                k,
+                pad_phi.at[pl.ds(1, nx), pl.ds(1, ny), :, lane_source(c)],
+                pad_phi.at[pl.ds(1, nx), pl.ds(1, ny), :, lane_target(c)],
+                send_phi,
+                recv_phi,
+            )
+        )
     for copy in copies:
+        copy.wait()
+    for copy in send_across(pad_phi, send_phi, recv_phi):
         copy.wait()
 
     def expand_phi(t, carry):

time: 47.5 us -> 49.5 us (1.042)
  Pallas kernels: 44 us -> 46 us
    pallas_call x1, Pallas kernels: 44 us -> 46 us  [body(): pl.pallas_call(functools.partial(kernel, (nx, ny, nz, slots), axis_sizes)...]
where the time goes in v2:
time: 49.5 us; the launch traced here: 49.2 us
  Pallas kernels  46 us (93%)
  local copies, waits for them, and re-layouts  1.65 us (3%)
  other arithmetic  1.49 us (3%)
    pallas_call x1, Pallas kernels, body(): pl.pallas_call(functools.partial(kernel, (nx, ny, nz, slots), axis_sizes)...  46 us

profile of v2, /device:TPU:0, one launch (start us, length us, event | category | flops | bytes accessed | tf_op | source)
XLA Modules:
  0.0 49.2 jit_solution(12173324809880159029)
XLA Ops:
  0.0 0.0 copy-start
  0.0 0.8 %broadcast_multiply_fusion = f32[3,3,8,96]{3,2,1,0:T(8,128)S(1)} fusion(f32[3,3,8,96]{3,2,1,0:T(8,128)} %param.2), kind=kLoop, calls=%fused_computation.2 | loop fusion | flops 6912 | bytes 55296 | tf_op jit(solution)/shard_map/mul | solution.py:291
  0.8 0.0 copy-done
  0.8 0.7 %pad_maximum_fusion.pay_ref = f32[3,3,8,128]{3,2,1,0:T(8,128)} fusion(f32[3,3,8,32]{3,2,1,0:T(8,128)S(1)} %select_select_fusion, f32[3,3,8,96]{3,2,1,0:T(8,128)S(1)} %broadcast_multiply_fusion), kind=kLoop, calls=%fused_computation | loop fusion | flops 9216 | bytes 73728 | tf_op jit(solution)/shard_map/concatenate | solution.py:291
  1.5 46.0 %shard_map.28 = f32[9,4,256]{2,1,0:T(4,128)} custom-call(f32[3,3,8,128]{3,2,1,0:T(8,128)} %pad_maximum_fusion.pay_ref), custom_call_target="tpu_custom_call" | custom-call | tf_op jit(solution)/shard_map/pallas_call | solution.py:294
  47.5 0.9 %reshape.6 = f32[3,3,4,8,32]{4,3,2,1,0:T(8,128)S(1)} reshape(f32[9,4,256]{2,1,0:T(4,128)} %shard_map.28) | data formatting | bytes 73728 | tf_op jit(solution)/shard_map/reshape | solution.py:319
  48.5 0.7 %reshape.7 = f32[3,3,8,128]{3,2,1,0:T(8,128)} reshape(f32[3,3,8,4,32]{4,3,2,1,0:T(4,128)S(1)} %copy.3) | data formatting | bytes 73728 | tf_op jit(solution)/shard_map/reshape | solution.py:320
  (2 shorter events, 0.0 us)
Async XLA Ops:
  0.0 0.8 %copy-start = (s32[3,3,8,32]{3,2,1,0:T(8,128)S(1)}, s32[3,3,8,32]{3,2,1,0:T(8,128)}, u32[]{:S(2)}) copy-start(s32[3,3,8,32]{3,2,1,0:T(8,128)} %param.3) | copy-start | bytes 27652
